TPU v7x, 128 devices: a whole 4x4x4 slice. The times are simulated.
128 devices in a mesh: pair: 16 (over x, z_lo, core), ga: 8 (over z_hi, y).
Axes of the slice: x: 4, y: 4, z: 4 (z_hi: 2, z_lo: 2; z = z_hi * 2 + z_lo), core: 2. Of those that a mesh axis runs over, the one named last changes fastest.
Arguments:
- densities: bfloat16 [24576, 4096], P('pair', 'ga'), may hold values from -6 to 6
- val_band: int32 [24576], P('pair'), may hold values from 0 to 127
- cond_band: int32 [24576], P('pair'), may hold values from 0 to 255
- val_energy: float32 [128], replicated, may hold values from -12 to -1
- cond_energy: float32 [256], replicated, may hold values from 1 to 12
Outputs:
- chi: float32 [4096, 4096], P('ga', 'pair')
All inputs are finite; a program needn't handle non-finite values.
Results may differ from a plain program's by a relative error of at most 0.0012.
Values may be sent and summed in bfloat16 or wider, within the bound.
A program may use at most 128 MiB of HBM per device.

v0:
```python
import math
import jax
import jax.numpy as jnp
from jax import lax
from jax.sharding import PartitionSpec as P


def lookup(bands, table):
    levels = lax.broadcasted_iota(jnp.int32, (1, table.shape[0]), 1)
    onehot = (bands[:, None] == levels).astype(jnp.float32)
    return jnp.sum(onehot * table[None, :], axis=1)


def per_device(densities, val_band, cond_band, val_energy, cond_energy):
    pairs_total = densities.shape[0] * lax.axis_size("pair")
    gap = lookup(val_band, val_energy) - lookup(cond_band, cond_energy)
    weight = 4.0 / (gap * math.sqrt(pairs_total))
    scaled = (weight[:, None] * densities.astype(jnp.float32)).astype(jnp.bfloat16)
    gathered = lax.all_gather(densities, "ga", axis=1, tiled=True)
    owned = lax.psum_scatter(
        lax.dot_general(
            gathered, scaled, (((0,), (0,)), ((), ())), preferred_element_type=jnp.float32
        ),
        "pair",
        scatter_dimension=0,
        tiled=True,
    )
    return owned.T


def solution(mesh):
    placed = (P("pair", "ga"), P("pair"), P("pair"), P(), P())
    return jax.shard_map(
        per_device, mesh=mesh, in_specs=placed, out_specs=P("ga", "pair"), check_vma=False
    )
```

profile of v0, /device:TPU:5, one launch (start us, length us, event | category | flops | bytes accessed | tf_op | source)
XLA Modules:
  0.0 290.0 jit_solution(14027633360789709186)
XLA Ops:
  6.5 0.0 copy-start
  6.5 0.0 copy-start.3
  6.5 0.0 copy-start.2
  6.5 0.0 copy-start.1
  6.5 0.0 all-gather.2.cloned.1.call-start
  6.6 0.7 all-gather.2.cloned.1.call-update
  7.3 0.0 reduce-scatter.2.cloned.1.call-start
  7.3 0.0 copy-done.3
  7.3 1.2 select_reduce_fusion.1
  8.5 0.0 copy-done.2
  8.5 0.0 copy-done.1
  8.5 0.5 select_reduce_fusion
  9.1 163.8 %all-gather.2.cloned.1.call-done = bf16[1536,4096]{1,0:T(8,128)(2,1)} async-done(((bf16[1536,512]{1,0:T(8,128)(2,1)}), bf16[1536,4096]{1,0:T(8,128)(2,1)}) %all-gather.2.cloned.1.call-update) | async-done | bytes 12582928 | tf_op jit(solution)/shard_map/all_gather | solution.py:19
  172.9 0.0 copy-done
  172.9 12.0 %convolution_bitcast_fusion = f32[4096,512]{0,1:T(8,128)} fusion(bf16[1536,4096]{1,0:T(8,128)(2,1)} %all-gather.2.cloned.1.call-done, bf16[1536,512]{1,0:T(8,128)(2,1)S(1)} %copy-done, f32[1536]{0:T(1024)S(1)} %multiply_divide_fusion), kind=kOutput, calls=%fused_computation | convolution fusion | flops 6444810240 | bytes 22550528 | tf_op jit(solution)/shard_map/dot_general | solution.py:21
  184.9 0.0 reduce-scatter.2.cloned.1.call-update
  184.9 98.2 %reduce-scatter.2.cloned.1.call-done = f32[256,512]{0,1:T(8,128)} async-done(((f32[4096,512]{0,1:T(8,128)}), f32[256,512]{0,1:T(8,128)}) %reduce-scatter.2.cloned.1.call-update) | async-done | bytes 524304 | tf_op jit(solution)/shard_map/reduce_scatter | solution.py:20
  (1 shorter events, 0.0 us)
Async XLA Ops:
  6.5 166.4 %copy-start = (bf16[1536,512]{1,0:T(8,128)(2,1)S(1)}, bf16[1536,512]{1,0:T(8,128)(2,1)}, u32[]{:S(2)}) copy-start(bf16[1536,512]{1,0:T(8,128)(2,1)} %param.5) | copy-start | bytes 4718596
  6.5 0.8 copy-start.3
  6.5 2.0 copy-start.2
  6.5 2.0 copy-start.1
  6.5 166.4 %all-gather.2.cloned.1.call-start = ((), (), s32[]{:S(2)}) async-start(), calls=%async_computation.1 | async-start | bytes 14155776 | tf_op jit(solution)/shard_map/all_gather | solution.py:19
  7.3 275.9 %reduce-scatter.2.cloned.1.call-start = ((), (), s32[]{:S(2)}) async-start(), calls=%async_computation.2 | async-start | bytes 8912896 | tf_op jit(solution)/shard_map/reduce_scatter | solution.py:20
Sparse Core Ops, SparseCore 0:
  9.5 163.3 all-gather.1
  185.1 98.0 reduce-scatter.1
where the time goes:
time: 290 us
  waiting for transfers between devices  263 us (91%)
  between operations  13.4 us (5%)
  matrix products  12 us (4%)
    all_gather x1, waiting for transfers between devices, per_device(): gathered = lax.all_gather(densities, 'ga', axis=1, tiled=True)  164 us
    reduce_scatter x1, waiting for transfers between devices, per_device(): lax.psum_scatter(lax.dot_general(gathered, scaled, (((0,), (0,)), ((), ()...  98.2 us
    dot_general x1, matrix products, per_device(): lax.dot_general(gathered, scaled, (((0,), (0,)), ((), ())), preferred_ele...  12 us
  transfers between devices with their start and end apart: 2, of which 2 were waited for; matrix products, arithmetic and copies ran while one was open for 1% of the time, Pallas kernels for 0%

commit v1 on v0

--- a/solution.py
+++ b/solution.py
@@ -3,6 +3,12 @@
 import jax.numpy as jnp
 from jax import lax
 from jax.sharding import PartitionSpec as P
+
+
+def settle_shifts_all_by_axis(buf):
+    z = jnp.stack([buf for _ in range(lax.psum(1, "ga"))], 0)
+    seen_now = lax.all_to_all(z, axis_name="ga", split_axis=0, concat_axis=0)
+    return jnp.concatenate(seen_now, 1)
 
 
 def lookup(bands, table):
@@ -16,7 +22,7 @@
     gap = lookup(val_band, val_energy) - lookup(cond_band, cond_energy)
     weight = 4.0 / (gap * math.sqrt(pairs_total))
     scaled = (weight[:, None] * densities.astype(jnp.float32)).astype(jnp.bfloat16)
-    gathered = lax.all_gather(densities, "ga", axis=1, tiled=True)
+    gathered = settle_shifts_all_by_axis(densities)
     owned = lax.psum_scatter(
         lax.dot_general(
             gathered, scaled, (((0,), (0,)), ((), ())), preferred_element_type=jnp.float32

time: 290 us -> 328 us (1.13)
  waiting for transfers between devices: 263 us -> 286 us
  starting transfers between devices: 0.07 us -> 7.68 us
  local copies, waits for them, and re-layouts: 0.01 us -> 7.27 us
    all_gather x1 -> x0, waiting for transfers between devices: 164 us -> none  [per_device(): gathered = lax.all_gather(densities, 'ga', axis=1, tiled=True)]
    all_to_all x0 -> x1, waiting for transfers between devices: none -> 140 us  [settle_shifts_all_by_axis(): seen_now = lax.all_to_all(z, axis_name='ga', split_axis=0, concat_axis=0)]
    reduce_scatter x1, waiting for transfers between devices: 98.2 us -> 146 us  [per_device(): lax.psum_scatter(lax.dot_general(gathered, scaled, (((0,), (0,)), ((), ()...]
    all_to_all x0 -> x1, starting transfers between devices: none -> 7.65 us  [settle_shifts_all_by_axis(): seen_now = lax.all_to_all(z, axis_name='ga', split_axis=0, concat_axis=0)]
    another operation x0 -> x1, local copies, waits for them, and re-layouts: none -> 5.54 us  [settle_shifts_all_by_axis(): z = jnp.stack([buf for _ in range(lax.psum(1, 'ga'))], 0)]
  transfers between devices with their start and end apart: 2 -> 2, of which waited for: 2 -> 2; matrix products, arithmetic and copies ran while one was open for 1% -> 0% of each run, Pallas kernels for 0% -> 0%
where the time goes in v1:
time: 328 us
  waiting for transfers between devices  286 us (87%)
  between operations  13.5 us (4%)
  matrix products  12.3 us (4%)
  starting transfers between devices  7.68 us (2%)
  local copies, waits for them, and re-layouts  7.27 us (2%)
    reduce_scatter x1, waiting for transfers between devices, per_device(): lax.psum_scatter(lax.dot_general(gathered, scaled, (((0,), (0,)), ((), ()...  146 us
    all_to_all x1, waiting for transfers between devices, settle_shifts_all_by_axis(): seen_now = lax.all_to_all(z, axis_name='ga', split_axis=0, concat_axis=0)  140 us
    dot_general x1, matrix products, per_device(): lax.dot_general(gathered, scaled, (((0,), (0,)), ((), ())), preferred_ele...  12.3 us
    all_to_all x1, starting transfers between devices, settle_shifts_all_by_axis(): seen_now = lax.all_to_all(z, axis_name='ga', split_axis=0, concat_axis=0)  7.65 us
  transfers between devices with their start and end apart: 2, of which 2 were waited for; matrix products, arithmetic and copies ran while one was open for 0% of the time, Pallas kernels for 0%

profile of v1, /device:TPU:5, one launch (start us, length us, event | category | flops | bytes accessed | tf_op | source)
XLA Modules:
  0.0 327.6 jit_solution(101814148786205377)
XLA Ops:
  6.5 1.7 copy.7
  8.3 5.5 %stack.2 = bf16[8,1536,512]{1,2,0:T(8,128)(2,1)} broadcast(bf16[1536,512]{0,1:T(8,128)(2,1)S(1)} %copy.7), dimensions={1,2} | broadcast | bytes 14155776 | tf_op jit(solution)/shard_map/stack | solution.py:9
  13.8 0.0 copy-start.1
  13.8 0.0 copy-start.4
  13.8 0.0 copy-start.2
  13.8 0.0 copy-start.3
  13.8 0.0 copy-start
  13.8 7.6 %all-to-all-start = ((bf16[8,1536,512]{1,2,0:T(8,128)(2,1)}), bf16[8,1536,512]{1,2,0:T(8,128)(2,1)}, u32[]{:S(2)}, u32[]{:S(2)}) async-start(bf16[8,1536,512]{1,2,0:T(8,128)(2,1)} %stack.2), calls=%async_computation | async-start | bytes 25165824 | tf_op jit(solution)/shard_map/all_to_all | solution.py:10
  21.5 0.0 reduce-scatter.2.cloned.1.call-start
  21.5 0.0 copy-done.1
  21.5 0.0 copy-done.4
  21.5 0.5 select_reduce_fusion.1
  22.0 0.0 copy-done.2
  22.0 0.0 copy-done.3
  22.0 0.5 select_reduce_fusion
  22.6 140.0 %all-to-all-done = bf16[8,1536,512]{1,2,0:T(8,128)(2,1)} async-done(((bf16[8,1536,512]{1,2,0:T(8,128)(2,1)}), bf16[8,1536,512]{1,2,0:T(8,128)(2,1)}, u32[]{:S(2)}, u32[]{:S(2)}) %all-to-all-start) | async-done | bytes 12582944 | tf_op jit(solution)/shard_map/all_to_all | solution.py:10
  162.5 0.0 copy-done
  162.5 12.3 %convolution_bitcast_fusion = f32[4096,512]{0,1:T(8,128)} fusion(bf16[1536,4096]{0,1:T(8,128)(2,1)} %bitcast.1, bf16[1536,512]{1,0:T(8,128)(2,1)S(1)} %copy-done, f32[1536]{0:T(1024)S(1)} %multiply_divide_fusion), kind=kOutput, calls=%fused_computation | convolution fusion | flops 6444810240 | bytes 22550528 | tf_op jit(solution)/shard_map/dot_general | solution.py:27
  174.8 0.0 reduce-scatter.2.cloned.1.call-update
  174.9 145.9 %reduce-scatter.2.cloned.1.call-done = f32[256,512]{0,1:T(8,128)} async-done(((f32[4096,512]{0,1:T(8,128)}), f32[256,512]{0,1:T(8,128)}) %reduce-scatter.2.cloned.1.call-update) | async-done | bytes 524304 | tf_op jit(solution)/shard_map/reduce_scatter | solution.py:26
  (1 shorter events, 0.0 us)
Async XLA Ops:
  13.8 7.7 %copy-start.1 = (s32[1536]{0:T(1024)S(1)}, s32[1536]{0:T(1024)}, u32[]{:S(2)}) copy-start(s32[1536]{0:T(1024)} %param.6) | copy-start | bytes 18436
  13.8 7.7 %copy-start.4 = (f32[128]{0:T(128)S(1)}, f32[128]{0:T(128)}, u32[]{:S(2)}) copy-start(f32[128]{0:T(128)} %param.8) | copy-start | bytes 1540
  13.8 8.2 %copy-start.2 = (s32[1536]{0:T(1024)S(1)}, s32[1536]{0:T(1024)}, u32[]{:S(2)}) copy-start(s32[1536]{0:T(1024)} %param.7) | copy-start | bytes 18436
  13.8 8.2 %copy-start.3 = (f32[256]{0:T(256)S(1)}, f32[256]{0:T(256)}, u32[]{:S(2)}) copy-start(f32[256]{0:T(256)} %param.9) | copy-start | bytes 3076
  13.8 148.7 %copy-start = (bf16[1536,512]{1,0:T(8,128)(2,1)S(1)}, bf16[1536,512]{1,0:T(8,128)(2,1)}, u32[]{:S(2)}) copy-start(bf16[1536,512]{1,0:T(8,128)(2,1)} %param.5) | copy-start | bytes 4718596
  13.8 148.7 %all-to-all-start = ((bf16[8,1536,512]{1,2,0:T(8,128)(2,1)}), bf16[8,1536,512]{1,2,0:T(8,128)(2,1)}, u32[]{:S(2)}, u32[]{:S(2)}) async-start(bf16[8,1536,512]{1,2,0:T(8,128)(2,1)} %stack.2), calls=%async_computation | async-start | bytes 25165824 | tf_op jit(solution)/shard_map/all_to_all | solution.py:10
  21.5 299.3 %reduce-scatter.2.cloned.1.call-start = ((), (), s32[]{:S(2)}) async-start(), calls=%async_computation.2 | async-start | bytes 8912896 | tf_op jit(solution)/shard_map/reduce_scatter | solution.py:26
Sparse Core Ops, SparseCore 0:
  175.0 145.7 reduce-scatter.1
